TPU v7x, 32 devices: a whole 2x2x4 slice. The times are simulated.
32 devices in a mesh: league: 2 (over x), seq: 16 (over z, y, core).
Axes of the slice: x: 2, y: 2, z: 4, core: 2. Of those that a mesh axis runs over, the one named last changes fastest.
Arguments:
- queries: bfloat16 [6144, 1792], P(('league', 'seq')), parts along dimension 0, may hold values from -100 to 100
- key_rows: bfloat16 [6144, 256], P(('league', 'seq')), parts along dimension 0, may hold values from -4 to 4
- value_rows: bfloat16 [6144, 256], P(('league', 'seq')), parts along dimension 0, may hold values from -6 to 6
- residual: bfloat16 [6144, 3584], P(('league', 'seq')), parts along dimension 0, may hold values from -6 to 6
- out_weight: bfloat16 [1792, 3584], P('seq'), may hold values from -0.125 to 0.125
- norm_gain: float32 [3584], replicated, may hold values from 0.1 to 1.9
- value_head: float32 [3584], replicated, may hold values from -0.09375 to 0.09375
- valid_length: int32 [2], P('league'), parts along dimension 0, may hold values from 1537 to 3072
Outputs:
- stream: bfloat16 [6144, 3584], P(('league', 'seq')), parts along dimension 0
- values: float32 [6144], P(('league', 'seq')), parts along dimension 0
There are 2 independent parts, one for each index of `league`. A program takes and returns all parts, laid end to end along the dimension named above; an argument that names none is the same for every part. Nothing has to cross between parts.
All inputs are finite; a program needn't handle non-finite values.
Results may differ from a plain program's by a relative error of at most 0.0085.
Values may be sent and summed in bfloat16 or wider, within the bound.
A program may use at most 128 MiB of HBM per device.

v0:
```python
import math

import jax
import jax.numpy as jnp
from jax import lax
from jax.sharding import PartitionSpec as P

HEAD_DIM = 128


NEG_BIG = -1e30


def row_positions(row_index, tok_count):
    owner_dev = row_index // tok_count
    within = row_index % tok_count
    return owner_dev * tok_count + within


def attend_block(
    carried, key_block, value_block, key_pos, query_grid, query_pos, query_limit, score_scale
):

    def run_block(carry_in):
        running_max, running_sum, running_out = carry_in
        scores = (
            jnp.einsum("qgrd,kgd->qgrk", query_grid, key_block, preferred_element_type=jnp.float32)
            * score_scale
        )
        allowed = key_pos[None, None, None, :] <= query_pos[:, None, None, None]
        new_max = jnp.maximum(running_max, jnp.max(jnp.where(allowed, scores, NEG_BIG), axis=-1))
        shrink = jnp.exp(running_max - new_max)
        weights = jnp.where(allowed, jnp.exp(scores - new_max[..., None]), 0.0)
        running_sum = running_sum * shrink + jnp.sum(weights, axis=-1)
        running_out = running_out * shrink[..., None] + jnp.einsum(
            "qgrk,kgd->qgrd",
            weights.astype(jnp.bfloat16),
            value_block,
            preferred_element_type=jnp.float32,
        )
        return (new_max, running_sum, running_out)

    def keep_block(carry_in):
        return carry_in

    needed = jnp.min(key_pos) <= query_limit
    return lax.cond(needed, run_block, keep_block, carried)


def attend_piece(
    carried, key_piece, value_piece, key_pos, query_grid, query_pos, query_limit, score_scale
):
    piece_rows = key_piece.shape[0]
    block_rows = math.gcd(piece_rows, 512)
    block_count = piece_rows // block_rows
    groups = key_piece.shape[1] // HEAD_DIM
    key_blocks = key_piece.reshape(block_count, block_rows, groups, HEAD_DIM)
    value_blocks = value_piece.reshape(block_count, block_rows, groups, HEAD_DIM)
    pos_blocks = key_pos.reshape(block_count, block_rows)

    def one_block(carry_in, inputs):
        return (
            attend_block(
                carry_in,
                inputs[0],
                inputs[1],
                inputs[2],
                query_grid,
                query_pos,
                query_limit,
                score_scale,
            ),
            None,
        )

    carried, unused = lax.scan(one_block, carried, (key_blocks, value_blocks, pos_blocks))
    return carried


def per_device(
    queries, key_rows, value_rows, residual, out_weight, norm_gain, value_head, valid_length
):
    device = lax.axis_index("seq")
    tok_count = queries.shape[0]
    valid_upto = valid_length[0]
    groups = key_rows.shape[1] // HEAD_DIM
    repeats = queries.shape[1] // key_rows.shape[1]
    score_scale = HEAD_DIM ** (-0.5)
    local_rows = jnp.arange(tok_count, dtype=jnp.int32)
    query_pos = row_positions(device * tok_count + local_rows, tok_count)
    query_ok = query_pos < valid_upto
    query_limit = jnp.max(jnp.where(query_ok, query_pos, -1))
    query_grid = queries.reshape(tok_count, groups, repeats, HEAD_DIM)
    start_state = (
        jnp.full((tok_count, groups, repeats), NEG_BIG, jnp.float32),
        jnp.zeros((tok_count, groups, repeats), jnp.float32),
        jnp.zeros((tok_count, groups, repeats, HEAD_DIM), jnp.float32),
    )
    key_piece = lax.all_gather(key_rows, "seq", axis=0, tiled=True)
    key_pos = row_positions(jnp.arange(key_piece.shape[0], dtype=jnp.int32), tok_count)
    carried = attend_piece(
        start_state,
        key_piece,
        lax.all_gather(value_rows, "seq", axis=0, tiled=True),
        key_pos,
        query_grid,
        query_pos,
        query_limit,
        score_scale,
    )
    running_max, running_sum, running_out = carried
    safe_sum = jnp.where(query_ok[:, None, None], running_sum, 1.0)
    attended = jnp.where(query_ok[:, None, None, None], running_out / safe_sum[..., None], 0.0)
    attended = attended.reshape(tok_count, groups * repeats * HEAD_DIM).astype(jnp.bfloat16)
    whole_weight = lax.all_gather(out_weight, "seq", axis=0, tiled=True)
    projected = jnp.dot(attended, whole_weight, preferred_element_type=jnp.float32)
    stream = (residual.astype(jnp.float32) + projected).astype(jnp.bfloat16)
    widened = stream.astype(jnp.float32)
    normed = widened * lax.rsqrt(jnp.mean(widened * widened, axis=-1, keepdims=True) + 1e-06)
    scored = jnp.sum(normed * (norm_gain * value_head)[None, :], axis=-1)
    natural_pos = device * tok_count + local_rows
    scored = jnp.where(natural_pos < valid_upto, scored, 0.0)
    return (stream, scored)


def solution(mesh):
    placed = (
        P(("league", "seq"), None),
        P(("league", "seq"), None),
        P(("league", "seq"), None),
        P(("league", "seq"), None),
        P("seq", None),
        P(),
        P(),
        P("league"),
    )
    return jax.shard_map(
        per_device,
        mesh=mesh,
        in_specs=placed,
        out_specs=(P(("league", "seq"), None), P(("league", "seq"))),
        check_vma=False,
    )
```

profile of v0, /device:TPU:25, one launch (start us, length us, event | category | flops | bytes accessed | tf_op | source)
XLA Modules:
  0.0 208.7 jit_solution(4323758560684722332)
XLA Ops:
  7.2 0.7 all-gather.4.cloned.1.call-update
  8.0 0.7 all-gather.6.cloned.1.call-update
  8.7 0.7 all-gather.8.cloned.1.call-update
  10.1 1.9 reshape.101
  12.2 0.6 select_reduce_fusion
  12.9 37.1 %all-gather.4.cloned.1.call-done = bf16[3072,256]{1,0:T(8,128)(2,1)} async-done(((bf16[192,256]{1,0:T(8,128)(2,1)}), bf16[3072,256]{1,0:T(8,128)(2,1)}) %all-gather.4.cloned.1.call-update) | async-done | bytes 1572880 | tf_op jit(solution)/shard_map/all_gather | solution.py:99
  50.0 2.4 %reshape.100 = bf16[6,512,2,128]{3,2,1,0:T(2,128)(2,1)S(1)} reshape(bf16[3072,256]{1,0:T(8,128)(2,1)} %all-gather.4.cloned.1.call-done) | data formatting | bytes 3145728 | tf_op jit(solution)/shard_map/reshape | solution.py:57
  52.4 1.4 copy.10
  53.8 36.8 %all-gather.6.cloned.1.call-done = bf16[3072,256]{1,0:T(8,128)(2,1)} async-done(((bf16[192,256]{1,0:T(8,128)(2,1)}), bf16[3072,256]{1,0:T(8,128)(2,1)}) %all-gather.6.cloned.1.call-update) | async-done | bytes 1572880 | tf_op jit(solution)/shard_map/all_gather | solution.py:104
  90.6 2.4 %reshape.102 = bf16[6,512,2,128]{3,2,1,0:T(2,128)(2,1)S(1)} reshape(bf16[3072,256]{1,0:T(8,128)(2,1)} %all-gather.6.cloned.1.call-done) | data formatting | bytes 3145728 | tf_op jit(solution)/shard_map/reshape | solution.py:58
  93.0 1.4 copy.12
  94.5 12.9 %while.15 = (s32[]{:T(128)}, f32[192,2,7]{0,2,1:T(8,128)S(1)}, f32[192,2,7]{0,2,1:T(8,128)S(1)}, f32[192,2,7,128]{3,0,2,1:T(8,128)S(1)}, s32[6,512]{1,0:T(8,128)...) while((s32[]{:T(128)}, f32[192,2,7]{0,2,1:T(8,128)S(1)}, ...), condition=%wide.region_7.8_spmd.clone, body=%wide.region_1.7_spmd.clone.sunk | while | flops 720577664 | bytes 21064692 | solution.py:76
  94.5 0.7 fusion.52
  96.7 0.7 fusion.52
  98.8 0.7 fusion.52
  101.0 0.7 fusion.52
  103.1 0.7 fusion.52
  105.3 0.7 fusion.52
  107.9 0.5 copy.13
  108.4 0.7 convert_element_type.25
  109.1 84.1 %all-gather.8.cloned.1.call-done = bf16[1792,3584]{1,0:T(8,128)(2,1)} async-done(((bf16[112,3584]{1,0:T(8,128)(2,1)}), bf16[1792,3584]{1,0:T(8,128)(2,1)}) %all-gather.8.cloned.1.call-update) | async-done | bytes 12845072 | tf_op jit(solution)/shard_map/all_gather | solution.py:115
  193.2 7.8 %fusion.35 = (f32[192]{0:T(256)S(1)}, bf16[192,3584]{1,0:T(8,128)(2,1)S(1)}) fusion(bf16[192,1792]{1,0:T(8,128)(2,1)S(1)} %convert_element_type.25, bf16[1792,3584]{1,0:T(8,128)(2,1)} %all-gather.8.cloned.1.call-done, bf16[192,3584]{1,0:T(8,128)(2,1)} %param.15), kind=kOutput, calls=%fused_computation.42 | convolution fusion | flops 2470379264 | bytes 16286464 | tf_op jit(solution)/shard_map/dot_general | solution.py:116
  201.1 0.5 fusion.37
  201.6 0.6 compare_select_fusion
  (55 shorter events, 1.3 us)
Async XLA Ops:
  7.2 5.0 %copy-start.1 = (f32[3584]{0:T(1024)S(1)}, f32[3584]{0:T(1024)}, u32[]{:S(2)}) copy-start(f32[3584]{0:T(1024)} %param.17) | copy-start | bytes 43012
  7.2 5.0 %copy-start.2 = (f32[3584]{0:T(1024)S(1)}, f32[3584]{0:T(1024)}, u32[]{:S(2)}) copy-start(f32[3584]{0:T(1024)} %param.18) | copy-start | bytes 43012
  7.2 42.8 %all-gather.4.cloned.1.call-start = ((), (), s32[]{:S(2)}) async-start(), calls=%async_computation | async-start | bytes 1671168 | tf_op jit(solution)/shard_map/all_gather | solution.py:99
  7.9 82.7 %all-gather.6.cloned.1.call-start = ((), (), s32[]{:S(2)}) async-start(), calls=%async_computation.1 | async-start | bytes 1671168 | tf_op jit(solution)/shard_map/all_gather | solution.py:104
  8.7 184.6 %all-gather.8.cloned.1.call-start = ((), (), s32[]{:S(2)}) async-start(), calls=%async_computation.2 | async-start | bytes 13647872 | tf_op jit(solution)/shard_map/all_gather | solution.py:115
  201.0 1.1 copy-start
Sparse Core Ops, SparseCore 0:
  10.3 39.6 all-gather.3
  52.3 38.2 all-gather.5
  92.9 100.3 all-gather.7
where the time goes:
time: 212 us; the launch traced here: 209 us
  waiting for transfers between devices  160 us (75%)
  between operations  14.6 us (7%)
  local copies, waits for them, and re-layouts  11 us (5%)
  loops' own time  8.35 us (4%)
  matrix products  7.79 us (4%)
  other arithmetic  6.76 us (3%)
    all_gather x1, waiting for transfers between devices, per_device(): whole_weight = lax.all_gather(out_weight, 'seq', axis=0, tiled=True)  84.1 us
    all_gather x1, waiting for transfers between devices, per_device(): key_piece = lax.all_gather(key_rows, 'seq', axis=0, tiled=True)  37.1 us
    all_gather x1, waiting for transfers between devices, per_device(): lax.all_gather(value_rows, 'seq', axis=0, tiled=True)  36.8 us
    another operation x1, loops' own time, attend_piece(): lax.scan(one_block, carried, (key_blocks, value_blocks, pos_blocks))  8.27 us
    dot_general x1, matrix products, per_device(): jnp.dot(attended, whole_weight, preferred_element_type=jnp.float32)  7.79 us
    reduce_min x6, other arithmetic, attend_block(): needed = jnp.min(key_pos) <= query_limit  4.3 us
  transfers between devices with their start and end apart: 3, of which 3 were waited for; matrix products, arithmetic and copies ran while one was open for 8% of the time, Pallas kernels for 0%

commit v1 on v0

v1 whole, which is shorter than its diff:
```python
import functools
import math

import jax
import jax.numpy as jnp
from jax import lax
from jax.experimental import pallas as pl
from jax.experimental.pallas import tpu as pltpu
from jax.sharding import PartitionSpec as P

HEAD_DIM = 128
NEG_BIG = -1e30
CORES = 2
ROWS_Y = 2
PLANE = CORES * ROWS_Y

W_UP, W_DOWN, W_Y, W_X, W_CORE, W_CORE_X, KV_UP, KV_Y, KV_CORE = range(9)


def kernel(
    planes,
    valid_ref,
    q_hbm,
    key_hbm,
    value_hbm,
    residual_hbm,
    weight_hbm,
    gain_ref,
    stream_ref,
    values_ref,
    q_ref,
    kv,
    weight,
    residual,
    attended,
    row_max,
    row_sum,
    out_sum,
    send,
    recv,
    local,
):
    league = lax.axis_index("league")
    me = lax.axis_index("seq")
    z = me // PLANE
    y = (me // CORES) % ROWS_Y
    c = me % CORES
    tok, width = residual.shape
    share = (width * 11 // 28) // 128 * 128
    whole = pl.ds(0, width)

    def slot(zp, yp, cp):
        return zp * PLANE + yp * CORES + cp

    def near(dz=0, fy=False, fc=False):
        yy = 1 - y if fy else y
        cc = 1 - c if fc else c
        return (league, slot(z + dz, yy, cc))

    side = league % 2
    over_x = (league + 1 - 2 * side, me)
    mine = pl.ds(pl.multiple_of(side * share, 128), width - share)
    given = pl.ds(pl.multiple_of(side * (width - share), 128), share)
    taken = pl.ds(pl.multiple_of((1 - side) * (width - share), 128), share)

    def move(kind, zp, yp, cp, target, columns=None):
        index = zp * ROWS_Y + yp
        if kind in (KV_UP, KV_Y, KV_CORE):
            ref = kv.at[slot(zp, yp, cp)]
        else:
            ref = weight.at[slot(zp, yp, cp), :, columns]
        return pltpu.make_async_remote_copy(
            src_ref=ref,
            dst_ref=ref,
            send_sem=send.at[kind, index],
            recv_sem=recv.at[kind, index],
            device_id=target,
            device_id_type=pl.DeviceIdType.MESH,
        )

    other_core = near(fc=True)
    other_y = near(fy=True)
    up = (league, jnp.minimum(me + PLANE, planes * PLANE - 1))
    down = (league, jnp.maximum(me - PLANE, 0))
    has_up = z < planes - 1
    has_down = z > 0

    loads = [
        pltpu.make_async_copy(key_hbm, kv.at[me, :, pl.ds(0, key_hbm.shape[1])], local.at[0]),
        pltpu.make_async_copy(
            value_hbm, kv.at[me, :, pl.ds(key_hbm.shape[1], key_hbm.shape[1])], local.at[1]
        ),
        pltpu.make_async_copy(weight_hbm, weight.at[me], local.at[2]),
        pltpu.make_async_copy(q_hbm, q_ref, local.at[3]),
        pltpu.make_async_copy(residual_hbm, residual, local.at[4]),
    ]
    for load in loads:
        load.start()

    barrier = pltpu.get_barrier_semaphore()

    def greet(target):
        pl.semaphore_signal(
            barrier, inc=1, device_id=target, device_id_type=pl.DeviceIdType.MESH
        )

    greet(over_x)
    greet(other_y)
    greet(other_core)
    pl.when(has_up)(lambda: greet(up))
    pl.when(has_down)(lambda: greet(down))
    pl.semaphore_wait(barrier, 3 + has_up.astype(jnp.int32) + has_down.astype(jnp.int32))

    def spread_kv(zp):
        pl.when(has_up)(lambda: move(KV_UP, zp, y, c, up).start())
        move(KV_Y, zp, y, c, other_y).start()
        move(KV_CORE, zp, y, c, other_core).start()

    loads[0].wait()
    loads[1].wait()
    spread_kv(z)
    loads[2].wait()
    pl.when(has_down)(lambda: move(W_DOWN, z, y, c, down, mine).start())

    def kv_round(r, carry):
        @pl.when(jnp.logical_and(r >= 1, z - r >= 0))
        def _():
            move(KV_UP, z - r, y, c, up).wait_recv()
            spread_kv(z - r)

        @pl.when(jnp.logical_and(r >= 1, z - r + 1 >= 0))
        def _():
            move(KV_Y, z - r + 1, 1 - y, c, other_y).wait_recv()
            move(KV_CORE, z - r + 1, 1 - y, c, other_core).start()

        return carry

    lax.fori_loop(0, planes + 1, kv_round, 0)

    pl.when(has_up)(lambda: move(W_UP, z, y, c, up, mine).start())
    move(W_Y, z, y, c, other_y, mine).start()
    move(W_CORE, z, y, c, other_core, whole).start()
    loads[3].wait()

    heads = q_ref.shape[1] // HEAD_DIM
    groups = key_hbm.shape[1] // HEAD_DIM
    factor = HEAD_DIM ** (-0.5) * math.log2(math.e)
    row_max[...] = jnp.full(row_max.shape, NEG_BIG, jnp.float32)
    row_sum[...] = jnp.zeros(row_sum.shape, jnp.float32)
    out_sum[...] = jnp.zeros(out_sum.shape, jnp.float32)

    def attend(zp):
        for yp in (y, 1 - y):
            move(KV_CORE, zp, yp, 1 - c, other_core).wait_recv()
        keys = PLANE * tok
        query_pos = me * tok + lax.broadcasted_iota(jnp.int32, (tok, keys), 0)
        key_pos = zp * keys + lax.broadcasted_iota(jnp.int32, (tok, keys), 1)
        allowed = key_pos <= query_pos

        def one_head(h, carry):
            g = h // (heads // groups)
            q = q_ref[:, pl.ds(pl.multiple_of(h * HEAD_DIM, HEAD_DIM), HEAD_DIM)]
            at = pl.ds(zp * PLANE, PLANE)
            k = kv[at, :, pl.ds(pl.multiple_of(g * HEAD_DIM, HEAD_DIM), HEAD_DIM)]
            v = kv[at, :, pl.ds(pl.multiple_of((groups + g) * HEAD_DIM, HEAD_DIM), HEAD_DIM)]
            k = k.reshape(keys, HEAD_DIM)
            v = v.reshape(keys, HEAD_DIM)
            scores = lax.dot_general(
                q, k, (((1,), (1,)), ((), ())), preferred_element_type=jnp.float32
            )
            scores = jnp.where(allowed, scores * factor, NEG_BIG)
            old_max = row_max[h]
            new_max = jnp.maximum(old_max, jnp.max(scores, axis=1, keepdims=True))
            shrink = jnp.exp2(old_max - new_max)
            weights = jnp.exp2(scores - new_max)
            row_max[h] = new_max
            row_sum[h] = row_sum[h] * shrink + jnp.sum(weights, axis=1, keepdims=True)
            out_sum[h] = out_sum[h] * shrink + jnp.dot(
                weights.astype(jnp.bfloat16), v, preferred_element_type=jnp.float32
            )
            return carry

        lax.fori_loop(0, heads, one_head, 0)

    def onward(zp, yp):
        move(W_X, zp, yp, c, over_x, given).start()
        move(W_CORE, zp, yp, c, other_core, mine).start()

    def each_plane(r, body):
        pl.when(jnp.logical_and(r >= 0, z - r >= 0))(lambda: body(z - r))
        pl.when(jnp.logical_and(r >= 1, z + r < planes))(lambda: body(z + r))

    def weight_round(r, carry):
        @pl.when(jnp.logical_and(r >= 1, z - r >= 0))
        def _():
            move(W_UP, z - r, y, c, up, mine).wait_recv()
            pl.when(has_up)(lambda: move(W_UP, z - r, y, c, up, mine).start())
            move(W_Y, z - r, y, c, other_y, mine).start()
            onward(z - r, y)

        @pl.when(jnp.logical_and(r >= 1, z + r < planes))
        def _():
            move(W_DOWN, z + r, y, c, down, mine).wait_recv()
            pl.when(has_down)(lambda: move(W_DOWN, z + r, y, c, down, mine).start())
            move(W_Y, z + r, y, c, other_y, mine).start()
            onward(z + r, y)

        def from_y(zp):
            move(W_Y, zp, 1 - y, c, other_y, mine).wait_recv()
            onward(zp, 1 - y)

        each_plane(r - 1, from_y)

        def from_x(zp):
            def one(yp):
                move(W_X, zp, yp, c, over_x, taken).wait_recv()
                move(W_CORE_X, zp, yp, c, other_core, taken).start()

            pl.when(zp != z)(lambda: one(y))
            one(1 - y)

        each_plane(r - 2, from_x)
        pl.when(z - r >= 0)(lambda: attend(z - r))
        return carry

    lax.fori_loop(0, planes + 2, weight_round, 0)

    valid = valid_ref[0]
    rows = me * tok + lax.broadcasted_iota(jnp.int32, (tok, 1), 0)
    row_ok = rows < valid
    for h in range(heads):
        mixed = jnp.where(row_ok, out_sum[h] / jnp.where(row_ok, row_sum[h], 1.0), 0.0)
        attended[:, h * HEAD_DIM : (h + 1) * HEAD_DIM] = mixed.astype(jnp.bfloat16)
    loads[4].wait()

    def arrived(zp, carry):
        for yp in (y, 1 - y):
            own = jnp.logical_and(zp == z, yp == y)

            @pl.when(own)
            def _():
                move(W_CORE, zp, yp, 1 - c, other_core, whole).wait_recv()

            @pl.when(jnp.logical_not(own))
            def _():
                move(W_CORE, zp, yp, 1 - c, other_core, mine).wait_recv()
                move(W_CORE_X, zp, yp, 1 - c, other_core, taken).wait_recv()

        return carry

    lax.fori_loop(0, planes, arrived, 0)

    tile = math.gcd(width, 512)
    depth = weight.shape[1]
    count = weight.shape[0]

    def one_tile(t, carry):
        squares, dots = carry
        cols = pl.ds(pl.multiple_of(t * tile, tile), tile)
        if depth % 16 == 0:
            projected = jnp.dot(
                attended[...],
                weight[:, :, cols].reshape(count * depth, tile),
                preferred_element_type=jnp.float32,
            )
        else:
            projected = jnp.zeros((tok, tile), jnp.float32)
            for s in range(count):
                projected += jnp.dot(
                    attended[:, s * depth : (s + 1) * depth],
                    weight[s, :, cols],
                    preferred_element_type=jnp.float32,
                )
        stream = (residual[:, cols].astype(jnp.float32) + projected).astype(jnp.bfloat16)
        stream_ref[:, cols] = stream
        widened = stream.astype(jnp.float32)
        squares += jnp.sum(widened * widened, axis=1, keepdims=True)
        dots += jnp.sum(widened * gain_ref[:, cols], axis=1, keepdims=True)
        return squares, dots

    zero = jnp.zeros((tok, 1), jnp.float32)
    squares, dots = lax.fori_loop(0, width // tile, one_tile, (zero, zero))
    scored = dots * lax.rsqrt(squares / width + 1e-06)
    values_ref[...] = jnp.where(row_ok, scored, 0.0)

    def drain(zp, carry):
        @pl.when(zp <= z)
        def _():
            pl.when(has_up)(lambda: move(KV_UP, zp, y, c, up).wait_send())
            pl.when(has_up)(lambda: move(W_UP, zp, y, c, up, mine).wait_send())
            move(KV_Y, zp, y, c, other_y).wait_send()
            move(KV_CORE, zp, y, c, other_core).wait_send()
            move(KV_CORE, zp, 1 - y, c, other_core).wait_send()

        @pl.when(jnp.logical_and(zp >= z, has_down))
        def _():
            move(W_DOWN, zp, y, c, down, mine).wait_send()

        move(W_Y, zp, y, c, other_y, mine).wait_send()

        def sent(yp):
            move(W_X, zp, yp, c, over_x, given).wait_send()
            move(W_CORE, zp, yp, c, other_core, mine).wait_send()
            move(W_CORE_X, zp, yp, c, other_core, taken).wait_send()

        sent(1 - y)
        pl.when(zp != z)(lambda: sent(y))
        pl.when(zp == z)(lambda: move(W_CORE, zp, y, c, other_core, whole).wait_send())
        return carry

    lax.fori_loop(0, planes, drain, 0)


def per_device(
    devices,
    queries,
    key_rows,
    value_rows,
    residual,
    out_weight,
    norm_gain,
    value_head,
    valid_length,
):
    tok, q_width = queries.shape
    width = residual.shape[1]
    heads = q_width // HEAD_DIM
    planes = devices // PLANE
    any_space = pl.BlockSpec(memory_space=pl.ANY)
    vmem = pl.BlockSpec(memory_space=pltpu.VMEM)
    stream, scored = pl.pallas_call(
        functools.partial(kernel, planes),
        name="critic_block",
        out_shape=(
            jax.ShapeDtypeStruct((tok, width), jnp.bfloat16),
            jax.ShapeDtypeStruct((tok, 1), jnp.float32),
        ),
        in_specs=[pl.BlockSpec(memory_space=pltpu.SMEM)] + [any_space] * 5 + [vmem],
        out_specs=(vmem, vmem),
        scratch_shapes=[
            pltpu.VMEM((tok, q_width), jnp.bfloat16),
            pltpu.VMEM((devices, tok, 2 * key_rows.shape[1]), jnp.bfloat16),
            pltpu.VMEM((devices,) + out_weight.shape, jnp.bfloat16),
            pltpu.VMEM((tok, width), jnp.bfloat16),
            pltpu.VMEM((tok, q_width), jnp.bfloat16),
            pltpu.VMEM((heads, tok, 1), jnp.float32),
            pltpu.VMEM((heads, tok, 1), jnp.float32),
            pltpu.VMEM((heads, tok, HEAD_DIM), jnp.float32),
            pltpu.SemaphoreType.DMA((9, ROWS_Y * planes)),
            pltpu.SemaphoreType.DMA((9, ROWS_Y * planes)),
            pltpu.SemaphoreType.DMA((5,)),
        ],
        compiler_params=pltpu.CompilerParams(
            collective_id=0, has_side_effects=True, vmem_limit_bytes=60 * 1024 * 1024
        ),
    )(
        valid_length,
        queries,
        key_rows,
        value_rows,
        residual,
        out_weight,
        (norm_gain * value_head)[None, :],
    )
    return stream, scored[:, 0]


def solution(mesh):
    rows = P(("league", "seq"), None)
    return jax.shard_map(
        functools.partial(per_device, mesh.shape["seq"]),
        mesh=mesh,
        in_specs=(rows, rows, rows, rows, P("seq", None), P(), P(), P("league")),
        out_specs=(rows, P(("league", "seq"))),
        check_vma=False,
    )
```

time: 212 us -> 95.2 us (0.45); the launches traced: 209 us -> 94.8 us
  waiting for transfers between devices: 160 us -> 0 us
  Pallas kernels: 0 us -> 88 us
  between operations: 14.6 us -> 1.29 us
  loops' own time: 8.35 us -> 0 us
  local copies, waits for them, and re-layouts: 11 us -> 3.11 us
  matrix products: 7.79 us -> 0 us
  other arithmetic: 6.76 us -> 2.31 us
    all_gather x3 -> x0, waiting for transfers between devices: 158 us -> none  [the longest x1 84.1 us: per_device(): whole_weight = lax.all_gather(out_weight, 'seq', axis=0, tiled=True)]
    pallas_call x0 -> x1, Pallas kernels: none -> 88 us  [per_device(): pl.pallas_call(functools.partial(kernel, planes), name='critic_block', ou...]
    another operation x7 -> x0, loops' own time: 8.35 us -> none  [the longest x1 8.27 us: attend_piece(): lax.scan(one_block, carried, (key_blocks, value_blocks, pos_blocks))]
    dot_general x1 -> x0, matrix products: 7.79 us -> none  [per_device(): jnp.dot(attended, whole_weight, preferred_element_type=jnp.float32)]
    reshape x3 -> x0, local copies, waits for them, and re-layouts: 6.61 us -> none  [the longest x1 2.36 us: attend_piece(): key_blocks = key_piece.reshape(block_count, block_rows, groups, HEAD_DIM)]
    reduce_min x6 -> x0, other arithmetic: 4.3 us -> none  [attend_block(): needed = jnp.min(key_pos) <= query_limit]
  transfers between devices with their start and end apart: 3 -> 0, of which waited for: 3 -> 0; matrix products, arithmetic and copies ran while one was open for 8% -> 0% of each run, Pallas kernels for 0% -> 0%
where the time goes in v1:
time: 95.2 us; the launch traced here: 94.8 us
  Pallas kernels  88 us (92%)
  local copies, waits for them, and re-layouts  3.11 us (3%)
  other arithmetic  2.31 us (2%)
  between operations  1.29 us (1%)
    pallas_call x1, Pallas kernels, per_device(): pl.pallas_call(functools.partial(kernel, planes), name='critic_block', ou...  88 us
    unnamed x1, local copies, waits for them, and re-layouts  2.5 us

profile of v1, /device:TPU:25, one launch (start us, length us, event | category | flops | bytes accessed | tf_op | source)
XLA Modules:
  0.0 94.8 jit_solution(15173852157600960946)
XLA Ops:
  1.3 0.7 mul.3
  2.0 0.6 broadcast_in_dim.3.gain_ref
  2.6 88.0 %critic_block.1 = (bf16[192,3584]{1,0:T(8,128)(2,1)}, f32[192,1]{1,0:T(8,128)}) custom-call(s32[1]{0:T(128)S(6)} %copy.11.valid_ref, bf16[192,1792]{1,0:T(8,128)(2,1)} %q_hbm.1, bf16[192,256]{1,0:T(8,128)(2,1)} %key_hbm.1, bf16[192,256]{1,0:T(8,128)(2,1)} %value_hbm.1, bf16[192,3584]{1,0:T(8,128)(2,1)} %residual_hbm.1, bf16[112,3584]{1,0:T(8,128)(2,1)} %weight_hbm.1, ...), custom_call_target="tpu_custom_call" | custom-call | tf_op jit(solution)/shard_map/critic_block/pallas_call | solution.py:331
  90.7 1.6 %reduce = f32[192]{0:T(256)} reduce(f32[192,1]{1,0:T(8,128)} %get-tuple-element.5, f32[]{:T(128)} %constant.1), dimensions={1}, to_apply=%get-tuple-element.5.reduce_sub_computation | reduce | bytes 1540 | tf_op jit(solution)/shard_map/critic_block/pallas_call | solution.py:331
  92.3 2.5 %copy.12 = bf16[192,3584]{1,0:T(8,128)(2,1)} copy(bf16[192,3584]{1,0:T(8,128)(2,1)} %get-tuple-element.8) | data formatting | bytes 2752512

commit v2 on v1

--- a/solution.py
+++ b/solution.py
@@ -33,6 +33,7 @@
     weight,
     residual,
     attended,
+    projected,
     row_max,
     row_sum,
     out_sum,
@@ -118,29 +119,16 @@
 
     loads[0].wait()
     loads[1].wait()
-    spread_kv(z)
+    pl.when(has_up)(lambda: move(KV_UP, z, y, c, up).start())
+    move(KV_CORE, z, y, c, other_core).start()
     loads[2].wait()
+    move(W_Y, z, y, c, other_y, mine).start()
     pl.when(has_down)(lambda: move(W_DOWN, z, y, c, down, mine).start())
-
-    def kv_round(r, carry):
-        @pl.when(jnp.logical_and(r >= 1, z - r >= 0))
-        def _():
-            move(KV_UP, z - r, y, c, up).wait_recv()
-            spread_kv(z - r)
-
-        @pl.when(jnp.logical_and(r >= 1, z - r + 1 >= 0))
-        def _():
-            move(KV_Y, z - r + 1, 1 - y, c, other_y).wait_recv()
-            move(KV_CORE, z - r + 1, 1 - y, c, other_core).start()
-
-        return carry
-
-    lax.fori_loop(0, planes + 1, kv_round, 0)
-
     pl.when(has_up)(lambda: move(W_UP, z, y, c, up, mine).start())
-    move(W_Y, z, y, c, other_y, mine).start()
+    move(KV_Y, z, y, c, other_y).start()
     move(W_CORE, z, y, c, other_core, whole).start()
     loads[3].wait()
+    loads[4].wait()
 
     heads = q_ref.shape[1] // HEAD_DIM
     groups = key_hbm.shape[1] // HEAD_DIM
@@ -190,7 +178,65 @@
         pl.when(jnp.logical_and(r >= 0, z - r >= 0))(lambda: body(z - r))
         pl.when(jnp.logical_and(r >= 1, z + r < planes))(lambda: body(z + r))
 
+    def arrived(zp):
+        for yp in (y, 1 - y):
+            own = jnp.logical_and(zp == z, yp == y)
+
+            @pl.when(own)
+            def _():
+                move(W_CORE, zp, yp, 1 - c, other_core, whole).wait_recv()
+
+            @pl.when(jnp.logical_not(own))
+            def _():
+                move(W_CORE, zp, yp, 1 - c, other_core, mine).wait_recv()
+                move(W_CORE_X, zp, yp, 1 - c, other_core, taken).wait_recv()
+
+    tile = math.gcd(width, 512)
+    depth = weight.shape[1]
+
+    def project(zp):
+        arrived(zp)
+
+        def one_tile(t, carry):
+            cols = pl.ds(pl.multiple_of(t * tile, tile), tile)
+            rows = attended[zp]
+            if depth % 16 == 0:
+                block = weight[pl.ds(zp * PLANE, PLANE), :, cols]
+                projected[:, cols] += jnp.dot(
+                    rows,
+                    block.reshape(PLANE * depth, tile),
+                    preferred_element_type=jnp.float32,
+                )
+            else:
+                for i in range(PLANE):
+                    projected[:, cols] += jnp.dot(
+                        rows[:, i * depth : (i + 1) * depth],
+                        weight[zp * PLANE + i, :, cols],
+                        preferred_element_type=jnp.float32,
+                    )
+            return carry
+
+        lax.fori_loop(0, width // tile, one_tile, 0)
+
+    valid = valid_ref[0]
+    row_ok = me * tok + lax.broadcasted_iota(jnp.int32, (tok, 1), 0) < valid
+
+    def finish_attention():
+        parts = []
+        for h in range(heads):
+            mixed = out_sum[h] / jnp.where(row_ok, row_sum[h], 1.0)
+            parts.append(jnp.where(row_ok, mixed, 0.0).astype(jnp.bfloat16))
+        joined = jnp.concatenate(parts, axis=1)
+        for zp in range(planes):
+            attended[zp] = joined[:, zp * PLANE * depth : (zp + 1) * PLANE * depth]
+        projected[...] = residual[...].astype(jnp.float32)
+
     def weight_round(r, carry):
+        @pl.when(jnp.logical_and(r >= 1, z - r >= 0))
+        def _():
+            move(KV_UP, z - r, y, c, up).wait_recv()
+            spread_kv(z - r)
+
         @pl.when(jnp.logical_and(r >= 1, z - r >= 0))
         def _():
             move(W_UP, z - r, y, c, up, mine).wait_recv()
@@ -211,6 +257,11 @@
 
         each_plane(r - 1, from_y)
 
+        @pl.when(jnp.logical_and(r >= 1, z - r + 1 >= 0))
+        def _():
+            move(KV_Y, z - r + 1, 1 - y, c, other_y).wait_recv()
+            move(KV_CORE, z - r + 1, 1 - y, c, other_core).start()
+
         def from_x(zp):
             def one(yp):
                 move(W_X, zp, yp, c, over_x, taken).wait_recv()
@@ -220,58 +271,27 @@
             one(1 - y)
 
         each_plane(r - 2, from_x)
-        pl.when(z - r >= 0)(lambda: attend(z - r))
+        pl.when(jnp.logical_and(r >= 1, z - r + 1 >= 0))(lambda: attend(z - r + 1))
+
+        @pl.when(r == planes)
+        def _():
+            finish_attention()
+
+            def near_plane(d, carry):
+                each_plane(d, project)
+                return carry
+
+            lax.fori_loop(0, planes - 1, near_plane, 0)
+
         return carry
 
     lax.fori_loop(0, planes + 2, weight_round, 0)
-
-    valid = valid_ref[0]
-    rows = me * tok + lax.broadcasted_iota(jnp.int32, (tok, 1), 0)
-    row_ok = rows < valid
-    for h in range(heads):
-        mixed = jnp.where(row_ok, out_sum[h] / jnp.where(row_ok, row_sum[h], 1.0), 0.0)
-        attended[:, h * HEAD_DIM : (h + 1) * HEAD_DIM] = mixed.astype(jnp.bfloat16)
-    loads[4].wait()
-
-    def arrived(zp, carry):
-        for yp in (y, 1 - y):
-            own = jnp.logical_and(zp == z, yp == y)
-
-            @pl.when(own)
-            def _():
-                move(W_CORE, zp, yp, 1 - c, other_core, whole).wait_recv()
-
-            @pl.when(jnp.logical_not(own))
-            def _():
-                move(W_CORE, zp, yp, 1 - c, other_core, mine).wait_recv()
-                move(W_CORE_X, zp, yp, 1 - c, other_core, taken).wait_recv()
-
-        return carry
-
-    lax.fori_loop(0, planes, arrived, 0)
-
-    tile = math.gcd(width, 512)
-    depth = weight.shape[1]
-    count = weight.shape[0]
-
-    def one_tile(t, carry):
+    each_plane(planes - 1, project)
+
+    def finish_tile(t, carry):
         squares, dots = carry
         cols = pl.ds(pl.multiple_of(t * tile, tile), tile)
-        if depth % 16 == 0:
-            projected = jnp.dot(
-                attended[...],
-                weight[:, :, cols].reshape(count * depth, tile),
-                preferred_element_type=jnp.float32,
-            )
-        else:
-            projected = jnp.zeros((tok, tile), jnp.float32)
-            for s in range(count):
-                projected += jnp.dot(
-                    attended[:, s * depth : (s + 1) * depth],
-                    weight[s, :, cols],
-                    preferred_element_type=jnp.float32,
-                )
-        stream = (residual[:, cols].astype(jnp.float32) + projected).astype(jnp.bfloat16)
+        stream = projected[:, cols].astype(jnp.bfloat16)
         stream_ref[:, cols] = stream
         widened = stream.astype(jnp.float32)
         squares += jnp.sum(widened * widened, axis=1, keepdims=True)
@@ -279,7 +299,7 @@
         return squares, dots
 
     zero = jnp.zeros((tok, 1), jnp.float32)
-    squares, dots = lax.fori_loop(0, width // tile, one_tile, (zero, zero))
+    squares, dots = lax.fori_loop(0, width // tile, finish_tile, (zero, zero))
     scored = dots * lax.rsqrt(squares / width + 1e-06)
     values_ref[...] = jnp.where(row_ok, scored, 0.0)
 
@@ -342,7 +362,8 @@
             pltpu.VMEM((devices, tok, 2 * key_rows.shape[1]), jnp.bfloat16),
             pltpu.VMEM((devices,) + out_weight.shape, jnp.bfloat16),
             pltpu.VMEM((tok, width), jnp.bfloat16),
-            pltpu.VMEM((tok, q_width), jnp.bfloat16),
+            pltpu.VMEM((planes, tok, q_width // planes), jnp.bfloat16),
+            pltpu.VMEM((tok, width), jnp.float32),
             pltpu.VMEM((heads, tok, 1), jnp.float32),
             pltpu.VMEM((heads, tok, 1), jnp.float32),
             pltpu.VMEM((heads, tok, HEAD_DIM), jnp.float32),

time: 95.2 us -> 95.3 us (level)
  no operation moved by 1% of the time
where the time goes in v2:
time: 95.3 us; the launch traced here: 94.9 us
  Pallas kernels  88.2 us (93%)
  local copies, waits for them, and re-layouts  3.11 us (3%)
  other arithmetic  2.31 us (2%)
  between operations  1.29 us (1%)
    pallas_call x1, Pallas kernels, per_device(): pl.pallas_call(functools.partial(kernel, planes), name='critic_block', ou...  88.2 us
    unnamed x1, local copies, waits for them, and re-layouts  2.5 us

profile of v2, /device:TPU:25, one launch (start us, length us, event | category | flops | bytes accessed | tf_op | source)
XLA Modules:
  0.0 94.9 jit_solution(12688515408359205693)
XLA Ops:
  1.3 0.7 mul.3
  2.0 0.6 broadcast_in_dim.3.gain_ref
  2.6 88.2 %critic_block.1 = (bf16[192,3584]{1,0:T(8,128)(2,1)}, f32[192,1]{1,0:T(8,128)}) custom-call(s32[1]{0:T(128)S(6)} %copy.11.valid_ref, bf16[192,1792]{1,0:T(8,128)(2,1)} %q_hbm.1, bf16[192,256]{1,0:T(8,128)(2,1)} %key_hbm.1, bf16[192,256]{1,0:T(8,128)(2,1)} %value_hbm.1, bf16[192,3584]{1,0:T(8,128)(2,1)} %residual_hbm.1, bf16[112,3584]{1,0:T(8,128)(2,1)} %weight_hbm.1, ...), custom_call_target="tpu_custom_call" | custom-call | tf_op jit(solution)/shard_map/critic_block/pallas_call | solution.py:351
  90.8 1.6 %reduce = f32[192]{0:T(256)} reduce(f32[192,1]{1,0:T(8,128)} %get-tuple-element.5, f32[]{:T(128)} %constant.1), dimensions={1}, to_apply=%get-tuple-element.5.reduce_sub_computation | reduce | bytes 1540 | tf_op jit(solution)/shard_map/critic_block/pallas_call | solution.py:351
  92.4 2.5 %copy.12 = bf16[192,3584]{1,0:T(8,128)(2,1)} copy(bf16[192,3584]{1,0:T(8,128)(2,1)} %get-tuple-element.8) | data formatting | bytes 2752512

commit v3 on v2

--- a/solution.py
+++ b/solution.py
@@ -47,7 +47,7 @@
     y = (me // CORES) % ROWS_Y
     c = me % CORES
     tok, width = residual.shape
-    share = (width * 11 // 28) // 128 * 128
+    share = (width * 12 // 28) // 128 * 128
     whole = pl.ds(0, width)
 
     def slot(zp, yp, cp):

time: 95.3 us -> 94.6 us (level)
  Pallas kernels: 88.2 us -> 86.8 us
    pallas_call x1, Pallas kernels: 88.2 us -> 86.8 us  [per_device(): pl.pallas_call(functools.partial(kernel, planes), name='critic_block', ou...]
where the time goes in v3:
time: 94.6 us; the launch traced here: 93.5 us
  Pallas kernels  86.8 us (92%)
  local copies, waits for them, and re-layouts  3.11 us (3%)
  other arithmetic  2.31 us (2%)
  between operations  1.29 us (1%)
    pallas_call x1, Pallas kernels, per_device(): pl.pallas_call(functools.partial(kernel, planes), name='critic_block', ou...  86.8 us
    unnamed x1, local copies, waits for them, and re-layouts  2.5 us

profile of v3, /device:TPU:25, one launch (start us, length us, event | category | flops | bytes accessed | tf_op | source)
XLA Modules:
  0.0 93.5 jit_solution(5753810584765203080)
XLA Ops:
  1.3 0.7 mul.3
  2.0 0.6 broadcast_in_dim.3.gain_ref
  2.6 86.8 %critic_block.1 = (bf16[192,3584]{1,0:T(8,128)(2,1)}, f32[192,1]{1,0:T(8,128)}) custom-call(s32[1]{0:T(128)S(6)} %copy.11.valid_ref, bf16[192,1792]{1,0:T(8,128)(2,1)} %q_hbm.1, bf16[192,256]{1,0:T(8,128)(2,1)} %key_hbm.1, bf16[192,256]{1,0:T(8,128)(2,1)} %value_hbm.1, bf16[192,3584]{1,0:T(8,128)(2,1)} %residual_hbm.1, bf16[112,3584]{1,0:T(8,128)(2,1)} %weight_hbm.1, ...), custom_call_target="tpu_custom_call" | custom-call | tf_op jit(solution)/shard_map/critic_block/pallas_call | solution.py:351
  89.4 1.6 %reduce = f32[192]{0:T(256)} reduce(f32[192,1]{1,0:T(8,128)} %get-tuple-element.5, f32[]{:T(128)} %constant.1), dimensions={1}, to_apply=%get-tuple-element.5.reduce_sub_computation | reduce | bytes 1540 | tf_op jit(solution)/shard_map/critic_block/pallas_call | solution.py:351
  91.0 2.5 %copy.12 = bf16[192,3584]{1,0:T(8,128)(2,1)} copy(bf16[192,3584]{1,0:T(8,128)(2,1)} %get-tuple-element.8) | data formatting | bytes 2752512
